TPU v7x, 32 devices: a 4x4x1 block of a 4x4x8 slice. The times are simulated.
32 devices in a mesh: dp: 1 (over z), tp: 32 (over y, x, core).
Axes of the slice: x: 4, y: 4, z: 1, core: 2. Of those that a mesh axis runs over, the one named last changes fastest.
The devices are a block of a 4x4x8 slice.
Arguments:
- x_in: bfloat16 [8, 512, 4096], P('dp')
- adapter_ids: int32 [8], P('dp')
- gain_attn: float32 [4096], replicated
- gain_mlp: float32 [4096], replicated
- w_q: bfloat16 [4096, 32, 128], P(None, 'tp')
- w_k: bfloat16 [4096, 32, 128], P(None, 'tp')
- w_v: bfloat16 [4096, 32, 128], P(None, 'tp')
- w_o: bfloat16 [32, 128, 4096], P('tp')
- w_gate: bfloat16 [4096, 11008], P(None, 'tp')
- w_up: bfloat16 [4096, 11008], P(None, 'tp')
- w_down: bfloat16 [11008, 4096], P('tp')
- a_q: bfloat16 [4, 4096, 32], P(None, None, 'tp')
- b_q: bfloat16 [4, 32, 32, 128], P(None, None, 'tp')
- a_k: bfloat16 [4, 4096, 32], P(None, None, 'tp')
- b_k: bfloat16 [4, 32, 32, 128], P(None, None, 'tp')
- a_v: bfloat16 [4, 4096, 32], P(None, None, 'tp')
- b_v: bfloat16 [4, 32, 32, 128], P(None, None, 'tp')
- a_o: bfloat16 [4, 32, 128, 32], P(None, 'tp')
- b_o: bfloat16 [4, 32, 4096], P(None, None, 'tp')
- a_gate: bfloat16 [4, 4096, 32], P(None, None, 'tp')
- b_gate: bfloat16 [4, 32, 11008], P(None, None, 'tp')
- a_up: bfloat16 [4, 4096, 32], P(None, None, 'tp')
- b_up: bfloat16 [4, 32, 11008], P(None, None, 'tp')
- a_down: bfloat16 [4, 11008, 32], P(None, 'tp')
- b_down: bfloat16 [4, 32, 4096], P(None, None, 'tp')
Outputs:
- output: bfloat16 [8, 512, 4096], P('dp')
All inputs are finite; a program needn't handle non-finite values.
Results may differ from a plain program's by a relative error of at most 0.02.
Values are sent between devices in bfloat16 or wider.
A program may use at most 768 MiB of HBM per device.

v0:
```python
import jax
import jax.numpy as jnp
from jax import lax
from jax.sharding import PartitionSpec as P

value_a10 = 16
RMS_EPS = 1e-5


def rms_scale(x_in, gain_vec):
    x_f32 = x_in.astype(jnp.float32)
    inv_rms = lax.rsqrt(jnp.mean(x_f32 * x_f32, axis=-1, keepdims=True) + RMS_EPS)
    return (x_f32 * inv_rms * gain_vec).astype(jnp.bfloat16)


def causal_attention(q_flat, k_flat, v_flat, kv_heads, head_dim):
    num_seqs, seq_len = q_flat.shape[0], q_flat.shape[1]
    q_group = q_flat.reshape(num_seqs, seq_len, kv_heads, -1, head_dim)
    k_group = k_flat.reshape(num_seqs, seq_len, kv_heads, head_dim)
    v_group = v_flat.reshape(num_seqs, seq_len, kv_heads, head_dim)
    scores = jnp.einsum('bqngd,bknd->bngqk', q_group, k_group, preferred_element_type=jnp.float32) * head_dim ** -0.5
    causal = jnp.arange(seq_len)[:, None] >= jnp.arange(seq_len)[None, :]
    prob_bf = jax.nn.softmax(jnp.where(causal, scores, -jnp.inf), axis=-1).astype(jnp.bfloat16)
    att_out = jnp.einsum('bngqk,bknd->bqngd', prob_bf, v_group, preferred_element_type=jnp.float32)
    return att_out.astype(jnp.bfloat16).reshape(num_seqs, seq_len, -1)


def column_proj(h_in, w_loc, a_sel, b_sel, scale):
    value_a9 = jnp.einsum('bsd,bdr->bsr', h_in, a_sel, preferred_element_type=jnp.float32).astype(jnp.bfloat16)
    value_a8 = lax.all_gather(value_a9, 'tp', axis=2, tiled=True)
    base_out = jnp.einsum('bsd,de->bse', h_in, w_loc, preferred_element_type=jnp.float32)
    array_b8 = jnp.einsum('bsr,bre->bse', value_a8, b_sel, preferred_element_type=jnp.float32)
    return (base_out + scale * array_b8).astype(jnp.bfloat16)


def row_proj(h_in, w_loc, a_sel, b_sel, scale, resid_full):
    base_part = jnp.einsum('bse,ed->bsd', h_in, w_loc, preferred_element_type=jnp.float32).astype(jnp.bfloat16)
    value_a9 = jnp.einsum('bse,ber->bsr', h_in, a_sel, preferred_element_type=jnp.float32).astype(jnp.bfloat16)
    base_sum = lax.psum_scatter(base_part, 'tp', scatter_dimension=2, tiled=True)
    value_a8 = lax.psum(value_a9, 'tp')
    width = base_sum.shape[2]
    resid_loc = lax.dynamic_slice_in_dim(resid_full, lax.axis_index('tp') * width, width, axis=2)
    array_b8 = jnp.einsum('bsr,brd->bsd', value_a8, b_sel, preferred_element_type=jnp.float32)
    out_loc = resid_loc.astype(jnp.float32) + base_sum.astype(jnp.float32) + scale * array_b8
    return lax.all_gather(out_loc.astype(jnp.bfloat16), 'tp', axis=2, tiled=True)


def solution(mesh):
    act_spec = P('dp', None, None)
    w_head_spec = P(None, 'tp', None)
    w_out_spec = P('tp', None, None)
    w_col_spec = P(None, 'tp')
    w_row_spec = P('tp', None)
    a_rank_spec = P(None, None, 'tp')
    b_head_spec = P(None, None, 'tp', None)
    b_col_spec = P(None, None, 'tp')
    a_head_spec = P(None, 'tp', None, None)
    a_row_spec = P(None, 'tp', None)
    in_specs = (act_spec, P('dp'), P(None), P(None), w_head_spec, w_head_spec, w_head_spec, w_out_spec,
                w_col_spec, w_col_spec, w_row_spec, a_rank_spec, b_head_spec, a_rank_spec, b_head_spec,
                a_rank_spec, b_head_spec, a_head_spec, b_col_spec, a_rank_spec, b_col_spec,
                a_rank_spec, b_col_spec, a_row_spec, b_col_spec)

    def local_layer(x_in, adapter_ids, gain_attn, gain_mlp, w_q, w_k, w_v, w_o, w_gate, w_up, w_down,
                    a_q, b_q, a_k, b_k, a_v, b_v, a_o, b_o, a_gate, b_gate, a_up, b_up, a_down, b_down):
        num_seqs, model_dim = x_in.shape[0], x_in.shape[2]
        rank = b_q.shape[1]
        scale = value_a10 / rank

        def per_sequence(stack):
            return jnp.take(stack, adapter_ids, axis=0)

        def column(h_in, w_loc, a_stack, b_stack):
            return column_proj(h_in, w_loc.reshape(model_dim, -1), per_sequence(a_stack),
                               per_sequence(b_stack).reshape(num_seqs, rank, -1), scale)

        h_norm = rms_scale(x_in, gain_attn)
        q_loc = column(h_norm, w_q, a_q, b_q)
        k_loc = column(h_norm, w_k, a_k, b_k)
        v_loc = column(h_norm, w_v, a_v, b_v)
        att_loc = causal_attention(q_loc, k_loc, v_loc, w_k.shape[1], w_k.shape[2])
        x_one = row_proj(att_loc, w_o.reshape(-1, model_dim), per_sequence(a_o).reshape(num_seqs, -1, rank),
                         per_sequence(b_o), scale, x_in)
        h_two = rms_scale(x_one, gain_mlp)
        gate_loc = column(h_two, w_gate, a_gate, b_gate)
        up_loc = column(h_two, w_up, a_up, b_up)
        mlp_mid = (jax.nn.silu(gate_loc.astype(jnp.float32)) * up_loc.astype(jnp.float32)).astype(jnp.bfloat16)
        return row_proj(mlp_mid, w_down, per_sequence(a_down), per_sequence(b_down), scale, x_one)

    return jax.shard_map(local_layer, mesh=mesh, in_specs=in_specs, out_specs=act_spec, check_vma=False)
```

profile of v0, /device:TPU:97, one launch (start us, length us, event | category | flops | bytes accessed | tf_op | source)
XLA Modules:
  0.0 1345.3 jit_solution(1732924113857153759)
XLA Ops:
  8.3 11.4 fusion
  26.9 16.1 %fusion.70 = bf16[8,1,512]{2,1,0:T(2,128)(2,1)S(1)} fusion(bf16[8,4096,1]{1,0,2:T(8,128)(2,1)S(1)} %get-tuple-element.8, bf16[8,512,4096]{2,1,0:T(8,128)(2,1)} %param.33, f32[4096]{0:T(1024)} %param.35, f32[8,512]{1,0:T(8,128)} %add_rsqrt_fusion.1), kind=kOutput, calls=%fused_computation.87 | convolution fusion | flops 100663296 | bytes 33660928 | tf_op jit(solution)/shard_map/bsd,bdr->bsr/dot_general | solution.py:29
  43.1 14.1 %fusion.68 = bf16[8,1,512]{2,1,0:T(2,128)(2,1)S(1)} fusion(bf16[8,4096,1]{1,0,2:T(8,128)(2,1)S(1)} %get-tuple-element.10, bf16[8,512,4096]{2,1,0:T(8,128)(2,1)} %param.33, f32[4096]{0:T(1024)S(1)} %copy-done.25, f32[8,512]{1,0:T(8,128)S(1)} %copy-done.23), kind=kOutput, calls=%fused_computation.85 | convolution fusion | flops 100663296 | bytes 33660928 | tf_op jit(solution)/shard_map/bsd,bdr->bsr/dot_general | solution.py:29
  57.3 14.1 %fusion.72 = bf16[8,1,512]{2,1,0:T(2,128)(2,1)S(1)} fusion(bf16[8,4096,1]{1,0,2:T(8,128)(2,1)S(1)} %get-tuple-element.13, bf16[8,512,4096]{2,1,0:T(8,128)(2,1)} %param.33, f32[4096]{0:T(1024)S(1)} %copy-done.25, f32[8,512]{1,0:T(8,128)S(1)} %copy-done.23), kind=kOutput, calls=%fused_computation.89 | convolution fusion | flops 100663296 | bytes 33660928 | tf_op jit(solution)/shard_map/bsd,bdr->bsr/dot_general | solution.py:29
  71.4 32.5 %all_gather.21 = bf16[8,512,32]{1,0,2:T(8,128)(2,1)} all-gather(bf16[8,512,1]{1,0,2:T(8,128)(2,1)S(1)} %bitcast.195), channel_id=1, replica_groups=mesh['dp'=1,'tp'=32] {'tp'}, dimensions={2}, use_global_device_ids=true | all-gather | bytes 270336 | tf_op jit(solution)/shard_map/all_gather | solution.py:30
  103.9 33.3 %all_gather.23 = bf16[8,512,32]{1,0,2:T(8,128)(2,1)} all-gather(bf16[8,512,1]{1,0,2:T(8,128)(2,1)S(1)} %bitcast.192), channel_id=1, replica_groups=mesh['dp'=1,'tp'=32] {'tp'}, dimensions={2}, use_global_device_ids=true | all-gather | bytes 270336 | tf_op jit(solution)/shard_map/all_gather | solution.py:30
  137.2 33.1 %all_gather.22 = bf16[8,512,32]{1,0,2:T(8,128)(2,1)S(1)} all-gather(bf16[8,512,1]{1,0,2:T(8,128)(2,1)S(1)} %bitcast.191), channel_id=1, replica_groups=mesh['dp'=1,'tp'=32] {'tp'}, dimensions={2}, use_global_device_ids=true | all-gather | bytes 270336 | tf_op jit(solution)/shard_map/all_gather | solution.py:30
  170.3 16.5 %fusion.45 = f32[8,512,128]{2,1,0:T(8,128)} fusion(bf16[4096,1,128]{2,0,1:T(8,128)(2,1)} %param.38, bf16[8,512,4096]{2,1,0:T(8,128)(2,1)} %param.33, f32[4096]{0:T(1024)S(1)} %copy-done.25, f32[8,512]{1,0:T(8,128)S(1)} %copy-done.23), kind=kOutput, calls=%fused_computation.63 | convolution fusion | flops 4362076160 | bytes 36732928 | tf_op jit(solution)/shard_map/bsd,de->bse/dot_general | solution.py:31
  186.9 16.5 %fusion.43 = f32[8,512,128]{2,1,0:T(8,128)} fusion(bf16[4096,1,128]{2,0,1:T(8,128)(2,1)} %param.37, bf16[8,512,4096]{2,1,0:T(8,128)(2,1)} %param.33, f32[4096]{0:T(1024)S(1)} %copy-done.25, f32[8,512]{1,0:T(8,128)S(1)} %copy-done.23), kind=kOutput, calls=%fused_computation.61 | convolution fusion | flops 4362076160 | bytes 36732928 | tf_op jit(solution)/shard_map/bsd,de->bse/dot_general | solution.py:31
  203.4 16.9 %fusion.47 = f32[8,512,128]{2,1,0:T(8,128)} fusion(bf16[4096,1,128]{2,0,1:T(8,128)(2,1)} %param.39, bf16[8,512,4096]{2,1,0:T(8,128)(2,1)} %param.33, f32[4096]{0:T(1024)S(1)} %copy-done.25, f32[8,512]{1,0:T(8,128)S(1)} %copy-done.23), kind=kOutput, calls=%fused_computation.65 | convolution fusion | flops 4362076160 | bytes 36732928 | tf_op jit(solution)/shard_map/bsd,de->bse/dot_general | solution.py:31
  223.5 7.1 fusion.15
  235.8 8.0 fusion.38
  243.8 16.4 %convolution_convert_fusion.1 = bf16[8,512,4096]{2,1,0:T(8,128)(2,1)} fusion(bf16[8,512,128]{1,2,0:T(8,128)(2,1)} %fusion.38, bf16[1,128,4096]{2,1,0:T(8,128)(2,1)} %param.40), kind=kOutput, calls=%fused_computation.25 | convolution fusion | flops 4311744512 | bytes 35651584 | tf_op jit(solution)/shard_map/bse,ed->bsd/dot_general | solution.py:37
  260.2 43.8 %copy.57 = bf16[8,512,4096]{1,0,2:T(8,128)(2,1)} copy(bf16[8,512,4096]{2,1,0:T(8,128)(2,1)} %convolution_convert_fusion.1) | data formatting | bytes 67108864
  304.0 22.6 %copy.61 = bf16[512,8,8,512]{3,1,2,0:T(8,128)(2,1)} copy(bf16[512,8,8,512]{3,2,1,0:T(8,128)(2,1)} %bitcast.176) | data formatting | bytes 67108864
  330.9 156.3 %reduce-scatter.7.cloned.1.call-done = bf16[128,4096]{1,0:T(8,128)(2,1)} async-done(((bf16[4096,4096]{1,0:T(8,128)(2,1)}), bf16[128,4096]{1,0:T(8,128)(2,1)}) %reduce-scatter.7.cloned.1.call-update) | async-done | bytes 1048592
  492.5 90.9 %all-reduce.3.cloned.1.call-done = bf16[8,512,32]{1,2,0:T(8,128)(2,1)} async-done(((bf16[8,512,32]{1,2,0:T(8,128)(2,1)}), bf16[8,512,32]{1,2,0:T(8,128)(2,1)}) %all-reduce.3.cloned.1.call-update) | async-done | bytes 262160 | tf_op jit(solution)/shard_map/psum | solution.py:40
  587.9 117.1 %all-gather.3.cloned.1.call-done = bf16[8,512,4096]{2,1,0:T(8,128)(2,1)} async-done(((bf16[8,512,128]{2,1,0:T(8,128)(2,1)}), bf16[8,512,4096]{2,1,0:T(8,128)(2,1)}) %all-gather.3.cloned.1.call-update) | async-done | bytes 33554448 | tf_op jit(solution)/shard_map/all_gather | solution.py:45
  705.1 11.3 fusion.3
  716.5 14.2 %fusion.6 = bf16[8,1,512]{2,1,0:T(2,128)(2,1)S(1)} fusion(bf16[8,512,4096]{2,1,0:T(8,128)(2,1)} %all-gather.3.cloned.1.call-done, f32[4096]{0:T(1024)S(1)} %copy-done.26, f32[8,512]{1,0:T(8,128)S(1)} %add_rsqrt_fusion, bf16[8,4096,1]{1,0,2:T(8,128)(2,1)S(1)} %copy-done.19), kind=kOutput, calls=%fused_computation.26 | convolution fusion | flops 100663296 | bytes 33660928 | tf_op jit(solution)/shard_map/bsd,bdr->bsr/dot_general | solution.py:29
  730.6 14.1 %fusion.10 = bf16[8,1,512]{2,1,0:T(2,128)(2,1)S(1)} fusion(bf16[8,512,4096]{2,1,0:T(8,128)(2,1)} %all-gather.3.cloned.1.call-done, f32[4096]{0:T(1024)S(1)} %copy-done.26, f32[8,512]{1,0:T(8,128)S(1)} %add_rsqrt_fusion, bf16[8,4096,1]{1,0,2:T(8,128)(2,1)S(1)} %copy-done.18), kind=kOutput, calls=%fused_computation.28 | convolution fusion | flops 100663296 | bytes 33660928 | tf_op jit(solution)/shard_map/bsd,bdr->bsr/dot_general | solution.py:29
  744.8 28.3 %all_gather.26 = bf16[8,512,32]{1,0,2:T(8,128)(2,1)S(1)} all-gather(bf16[8,512,1]{1,0,2:T(8,128)(2,1)S(1)} %bitcast.193), channel_id=1, replica_groups=mesh['dp'=1,'tp'=32] {'tp'}, dimensions={2}, use_global_device_ids=true | all-gather | bytes 270336 | tf_op jit(solution)/shard_map/all_gather | solution.py:30
  773.2 33.0 %all_gather.25 = bf16[8,512,32]{1,0,2:T(8,128)(2,1)S(1)} all-gather(bf16[8,512,1]{1,0,2:T(8,128)(2,1)S(1)} %bitcast.194), channel_id=1, replica_groups=mesh['dp'=1,'tp'=32] {'tp'}, dimensions={2}, use_global_device_ids=true | all-gather | bytes 270336 | tf_op jit(solution)/shard_map/all_gather | solution.py:30
  808.9 18.1 %add_convert_fusion = bf16[8,512,344]{1,2,0:T(8,128)(2,1)} fusion(f32[8,512,344]{1,2,0:T(8,128)S(1)} %fusion.51, bf16[8,512,4096]{2,1,0:T(8,128)(2,1)} %all-gather.3.cloned.1.call-done, f32[4096]{0:T(1024)S(1)} %copy-done.26, f32[8,512]{1,0:T(8,128)S(1)} %add_rsqrt_fusion, bf16[4096,344]{0,1:T(8,128)(2,1)S(1)} %copy-done.24), kind=kOutput, calls=%fused_computation.41 | convolution fusion | flops 11614060544 | bytes 44859392 | tf_op jit(solution)/shard_map/bsd,de->bse/dot_general | solution.py:31
  827.0 18.7 %fusion.20 = bf16[8,512,344]{1,2,0:T(8,128)(2,1)S(1)} fusion(bf16[8,512,344]{1,2,0:T(8,128)(2,1)} %add_convert_fusion, f32[8,512,344]{1,2,0:T(8,128)S(1)} %fusion.53, bf16[4096,344]{0,1:T(8,128)(2,1)} %param.41, bf16[8,512,4096]{2,1,0:T(8,128)(2,1)} %all-gather.3.cloned.1.call-done, f32[4096]{0:T(1024)S(1)} %copy-done.26, f32[8,512]{1,0:T(8,128)S(1)} %add_rsqrt_fusion), kind=kOutput, calls=%fused_computation.43 | convolution fusion | flops 11625332736 | bytes 47677440 | tf_op jit(solution)/shard_map/bsd,de->bse/dot_general | solution.py:31
  847.3 22.0 %convolution_convert_fusion = bf16[8,512,4096]{2,1,0:T(8,128)(2,1)} fusion(bf16[8,512,344]{1,2,0:T(8,128)(2,1)S(1)} %fusion.20, bf16[344,4096]{1,0:T(8,128)(2,1)S(1)} %copy-done), kind=kOutput, calls=%fused_computation.24 | convolution fusion | flops 11559501824 | bytes 39190528 | tf_op jit(solution)/shard_map/bse,ed->bsd/dot_general | solution.py:37
  869.3 43.6 %copy.59 = bf16[8,512,4096]{1,0,2:T(8,128)(2,1)} copy(bf16[8,512,4096]{2,1,0:T(8,128)(2,1)} %convolution_convert_fusion) | data formatting | bytes 67108864
  912.9 22.9 %copy.63 = bf16[512,8,8,512]{3,1,2,0:T(8,128)(2,1)} copy(bf16[512,8,8,512]{3,2,1,0:T(8,128)(2,1)} %bitcast.177) | data formatting | bytes 67108864
  941.3 156.1 %reduce-scatter.9.cloned.1.call-done = bf16[128,4096]{1,0:T(8,128)(2,1)} async-done(((bf16[4096,4096]{1,0:T(8,128)(2,1)}), bf16[128,4096]{1,0:T(8,128)(2,1)}) %reduce-scatter.9.cloned.1.call-update) | async-done | bytes 1048592
  1102.6 90.7 %all-reduce.5.cloned.1.call-done = bf16[8,512,32]{1,2,0:T(8,128)(2,1)} async-done(((bf16[8,512,32]{1,2,0:T(8,128)(2,1)}), bf16[8,512,32]{1,2,0:T(8,128)(2,1)}) %all-reduce.5.cloned.1.call-update) | async-done | bytes 262160 | tf_op jit(solution)/shard_map/psum | solution.py:40
  1196.7 118.4 %all-gather.5.cloned.1.call-done = bf16[8,512,4096]{2,1,0:T(8,128)(2,1)} async-done(((bf16[8,512,128]{2,1,0:T(8,128)(2,1)}), bf16[8,512,4096]{2,1,0:T(8,128)(2,1)}) %all-gather.5.cloned.1.call-update) | async-done | bytes 33554448 | tf_op jit(solution)/shard_map/all_gather | solution.py:45
  1315.1 22.9 %copy.112 = bf16[8,512,4096]{2,1,0:T(8,128)(2,1)} copy(bf16[8,512,4096]{2,1,0:T(8,128)(2,1)} %all-gather.5.cloned.1.call-done) | data formatting | bytes 67108864
  (104 shorter events, 49.7 us)
Async XLA Ops:
  6.5 840.7 %copy-start = (bf16[344,4096]{1,0:T(8,128)(2,1)S(1)}, bf16[344,4096]{1,0:T(8,128)(2,1)}, u32[]{:S(2)}) copy-start(bf16[344,4096]{1,0:T(8,128)(2,1)} %param.43) | copy-start | bytes 8454148
  6.6 480.6 %reduce-scatter.7.cloned.1.call-start = ((), (), s32[]{:S(2)}) async-start(), calls=%async_computation.6 | async-start | bytes 34603008
  8.2 17.4 %copy-start.21 = (s32[1024]{0:T(1024)}, s32[1024]{0:T(1024)S(1)}, u32[]{:S(2)}) copy-start(s32[1024]{0:T(1024)S(1)} %pad_clamp_fusion) | copy-start | bytes 12292
  8.2 12.1 copy-start.1
  8.2 12.7 copy-start.2
  8.2 13.3 copy-start.13
  8.2 14.4 %copy-start.3 = (bf16[4,4096,1]{1,0,2:T(4,128)(2,1)S(1)}, bf16[4,4096,1]{1,0,2:T(4,128)(2,1)}, u32[]{:S(2)}) copy-start(bf16[4,4096,1]{1,0,2:T(4,128)(2,1)} %param.44) | copy-start | bytes 98308
  8.2 15.0 %copy-start.14 = (bf16[4,32,1,128]{3,1,2,0:T(8,128)(2,1)S(1)}, bf16[4,32,1,128]{3,1,2,0:T(8,128)(2,1)}, u32[]{:S(2)}) copy-start(bf16[4,32,1,128]{3,1,2,0:T(8,128)(2,1)} %param.47) | copy-start | bytes 98308
  8.2 15.6 %copy-start.4 = (bf16[4,4096,1]{1,0,2:T(4,128)(2,1)S(1)}, bf16[4,4096,1]{1,0,2:T(4,128)(2,1)}, u32[]{:S(2)}) copy-start(bf16[4,4096,1]{1,0,2:T(4,128)(2,1)} %param.46) | copy-start | bytes 98308
  8.2 16.2 %copy-start.15 = (bf16[4,32,1,128]{3,1,2,0:T(8,128)(2,1)S(1)}, bf16[4,32,1,128]{3,1,2,0:T(8,128)(2,1)}, u32[]{:S(2)}) copy-start(bf16[4,32,1,128]{3,1,2,0:T(8,128)(2,1)} %param.49) | copy-start | bytes 98308
  8.3 17.3 %copy-start.5 = (bf16[4,4096,1]{1,0,2:T(4,128)(2,1)S(1)}, bf16[4,4096,1]{1,0,2:T(4,128)(2,1)}, u32[]{:S(2)}) copy-start(bf16[4,4096,1]{1,0,2:T(4,128)(2,1)} %param.48) | copy-start | bytes 98308
  26.9 16.2 %copy-start.23 = (f32[8,512]{1,0:T(8,128)S(1)}, f32[8,512]{1,0:T(8,128)}, u32[]{:S(2)}) copy-start(f32[8,512]{1,0:T(8,128)} %add_rsqrt_fusion.1) | copy-start | bytes 49156
  26.9 16.2 %copy-start.25 = (f32[4096]{0:T(1024)S(1)}, f32[4096]{0:T(1024)}, u32[]{:S(2)}) copy-start(f32[4096]{0:T(1024)} %param.35) | copy-start | bytes 49156
  203.4 16.9 %copy-start.11 = (bf16[8,32,128]{2,1,0:T(8,128)(2,1)S(1)}, bf16[8,32,128]{2,1,0:T(8,128)(2,1)}, u32[]{:S(2)}) copy-start(bf16[8,32,128]{2,1,0:T(8,128)(2,1)} %gather_fusion.7) | copy-start | bytes 196612
  223.5 12.3 copy-start.20
  230.6 5.2 copy-start.12
  326.6 0.8 copy-start.22
  326.6 3.7 copy-start.16
  326.7 260.1 %copy-start.9 = (bf16[4,32,344]{2,1,0:T(8,128)(2,1)S(1)}, bf16[4,32,344]{2,1,0:T(8,128)(2,1)}, u32[]{:S(2)}) copy-start(bf16[4,32,344]{2,1,0:T(8,128)(2,1)} %param.55) | copy-start | bytes 264196
  326.7 260.7 %copy-start.10 = (bf16[4,32,344]{2,1,0:T(8,128)(2,1)S(1)}, bf16[4,32,344]{2,1,0:T(8,128)(2,1)}, u32[]{:S(2)}) copy-start(bf16[4,32,344]{2,1,0:T(8,128)(2,1)} %param.53) | copy-start | bytes 264196
  326.7 256.6 %all-reduce.3.cloned.1.call-start = ((), (), s32[]{:S(2)}) async-start(), calls=%async_computation.2 | async-start | bytes 524288 | tf_op jit(solution)/shard_map/psum | solution.py:40
  330.2 374.9 %all-gather.3.cloned.1.call-start = ((), (), s32[]{:S(2)}) async-start(), calls=%async_computation.3 | async-start | bytes 34603008 | tf_op jit(solution)/shard_map/all_gather | solution.py:45
  586.6 510.7 %reduce-scatter.9.cloned.1.call-start = ((), (), s32[]{:S(2)}) async-start(), calls=%async_computation.7 | async-start | bytes 34603008
  587.9 128.5 %copy-start.19 = (bf16[8,4096,1]{1,0,2:T(8,128)(2,1)S(1)}, bf16[8,4096,1]{1,0,2:T(8,128)(2,1)}, u32[]{:S(2)}) copy-start(bf16[8,4096,1]{1,0,2:T(8,128)(2,1)} %get-tuple-element.12) | copy-start | bytes 196612
  587.9 128.5 %copy-start.26 = (f32[4096]{0:T(1024)S(1)}, f32[4096]{0:T(1024)}, u32[]{:S(2)}) copy-start(f32[4096]{0:T(1024)} %param.36) | copy-start | bytes 49156
  716.5 14.2 %copy-start.18 = (bf16[8,4096,1]{1,0,2:T(8,128)(2,1)S(1)}, bf16[8,4096,1]{1,0,2:T(8,128)(2,1)}, u32[]{:S(2)}) copy-start(bf16[8,4096,1]{1,0,2:T(8,128)(2,1)} %get-tuple-element.6) | copy-start | bytes 196612
  744.8 64.1 %copy-start.24 = (bf16[4096,344]{0,1:T(8,128)(2,1)S(1)}, bf16[4096,344]{0,1:T(8,128)(2,1)}, u32[]{:S(2)}) copy-start(bf16[4096,344]{0,1:T(8,128)(2,1)} %param.42) | copy-start | bytes 8454148
  845.7 1.6 copy-start.7
  935.8 0.9 copy-start.6
  935.8 4.8 copy-start.17
  935.8 257.5 %all-reduce.5.cloned.1.call-start = ((), (), s32[]{:S(2)}) async-start(), calls=%async_computation.4 | async-start | bytes 524288 | tf_op jit(solution)/shard_map/psum | solution.py:40
  940.5 374.6 %all-gather.5.cloned.1.call-start = ((), (), s32[]{:S(2)}) async-start(), calls=%async_computation.5 | async-start | bytes 34603008 | tf_op jit(solution)/shard_map/all_gather | solution.py:45
  (1 other events, 0.8 us)
Sparse Core Ops, SparseCore 0:
  326.8 160.3 reduce-scatter.6
  490.5 92.7 all-reduce.2
  586.8 118.2 all-gather.2
  935.9 161.3 reduce-scatter.8
  1100.5 92.7 all-reduce.4
  1196.8 118.2 all-gather.4
where the time goes:
time: 1360 us; the launch traced here: 1350 us
  waiting for transfers between devices  730 us (54%)
  matrix products  231 us (17%)
  local copies, waits for them, and re-layouts  179 us (13%)
  blocking collectives  160 us (12%)
  other arithmetic  30.8 us (2%)
  between operations  14.4 us (1%)
    unnamed x8, waiting for transfers between devices  313 us
    all_gather x2, waiting for transfers between devices, row_proj(): lax.all_gather(out_loc.astype(jnp.bfloat16), 'tp', axis=2, tiled=True)  236 us
    psum x2, waiting for transfers between devices, row_proj(): value_a8 = lax.psum(value_a9, 'tp')  182 us
    unnamed x63, local copies, waits for them, and re-layouts  169 us
    all_gather x5, blocking collectives, column_proj(): value_a8 = lax.all_gather(value_a9, 'tp', axis=2, tiled=True)  160 us
    dot_general x5, matrix products, column_proj(): jnp.einsum('bsd,de->bse', h_in, w_loc, preferred_element_type=jnp.float32)  86.7 us
    dot_general x5, matrix products, column_proj(): jnp.einsum('bsd,bdr->bsr', h_in, a_sel, preferred_element_type=jnp.float32)  72.7 us
    dot_general x2, matrix products, row_proj(): jnp.einsum('bse,ed->bsd', h_in, w_loc, preferred_element_type=jnp.float32)  38.4 us
  transfers between devices with their start and end apart: 6, of which 6 were waited for; matrix products, arithmetic and copies ran while one was open for 1% of the time, Pallas kernels for 0%

commit v1 on v0

v1 whole, which is shorter than its diff:
```python
import functools

import jax
import jax.numpy as jnp
from jax import lax
from jax.experimental import pallas as pl
from jax.experimental.pallas import tpu as pltpu
from jax.sharding import PartitionSpec as P

LORA_ALPHA = 16
RMS_EPS = 1e-5
LANES = 128
CORES = 2
MESH = pl.DeviceIdType.MESH
PATTERNS = (('x', 'y', 1), ('x', 'y', -1), ('y', 'x', 1), ('y', 'x', -1))
RS_PARTS = (0, 1, 2, 3, 0)


class Torus:
    def __init__(self, side):
        me = lax.axis_index('tp')
        self.side = side
        self.core = lax.rem(me, CORES)
        self.x = lax.rem(me // CORES, side)
        self.y = me // (CORES * side)

    def pos(self, axis, step=0):
        here = self.x if axis == 'x' else self.y
        return lax.rem(here + (step + self.side), self.side)

    def dev(self, axis, step):
        row, col = (self.y, self.pos('x', step)) if axis == 'x' else (self.pos('y', step), self.x)
        return {'tp': (row * self.side + col) * CORES + self.core}

    def partner(self):
        return {'tp': (self.y * self.side + self.x) * CORES + 1 - self.core}

    def barrier(self):
        sem = pltpu.get_barrier_semaphore()
        others = [self.dev(axis, step) for axis in ('x', 'y') for step in (1, -1)] + [self.partner()]
        for other in others:
            pl.semaphore_signal(sem, inc=1, device_id=other, device_id_type=MESH)
        pl.semaphore_wait(sem, len(others))


def remote(src, dst, send_sem, recv_sem, device):
    return pltpu.make_async_remote_copy(src_ref=src, dst_ref=dst, send_sem=send_sem, recv_sem=recv_sem,
                                        device_id=device, device_id_type=MESH)


def along(ref, axis, index, cols):
    return ref.at[:, index, :, cols] if axis == 'x' else ref.at[index, :, :, cols]


class ReduceScatter:
    def __init__(self, torus, parts, far, near, run, far2, near2, run2, send_sems, recv_sems):
        self.t, self.parts = torus, parts
        self.one, self.two = (far, near, run), (far2, near2, run2)
        self.send_sems, self.recv_sems = send_sems, recv_sems

    def _own(self, q, step):
        first, _, sign = PATTERNS[RS_PARTS[q]]
        ref, col, _, width = self.parts[q]
        return along(ref, first, self.t.pos(first, step * sign), pl.ds(col, width))

    def _copy(self, q, stage, kind):
        first, second, sign = PATTERNS[RS_PARTS[q]]
        _, _, col, width = self.parts[q]
        cols = pl.ds(col, width)
        axis = first if stage == 0 else second
        slots = self.one if stage == 0 else self.two
        ahead = kind != 1
        if kind == 2:
            src = slots[0]
            src = src.at[:, :, cols] if stage == 0 else src.at[:, cols]
        elif stage == 0:
            src = self._own(q, 2 if kind == 0 else -1)
        else:
            src = self.one[2].at[self.t.pos(second, (2 if kind == 0 else -1) * sign), :, cols]
        dst = slots[kind]
        dst = dst.at[:, :, cols] if stage == 0 else dst.at[:, cols]
        index = (q * 2 + stage) * 3 + kind
        return remote(src, dst, self.send_sems.at[index], self.recv_sems.at[index],
                      self.t.dev(axis, sign if ahead else -sign))

    def begin(self, q):
        self._copy(q, 0, 0).start()
        self._copy(q, 0, 1).start()

    def relay(self, q):
        self._copy(q, 0, 0).wait_recv()
        _, _, col, width = self.parts[q]
        cols = pl.ds(col, width)
        far = self.one[0]
        far[:, :, cols] = (far[:, :, cols].astype(jnp.float32) + self._own(q, 1)[...].astype(jnp.float32)).astype(far.dtype)
        self._copy(q, 0, 2).start()

    def turn(self, q):
        self._copy(q, 0, 1).wait_recv()
        self._copy(q, 0, 2).wait_recv()
        _, _, col, width = self.parts[q]
        cols = pl.ds(col, width)
        _, near, run = self.one
        total = run[:, :, cols].astype(jnp.float32) + near[:, :, cols].astype(jnp.float32)
        run[:, :, cols] = (total + self._own(q, 0)[...].astype(jnp.float32)).astype(run.dtype)
        self._copy(q, 1, 0).start()
        self._copy(q, 1, 1).start()

    def relay_two(self, q):
        _, second, sign = PATTERNS[RS_PARTS[q]]
        self._copy(q, 1, 0).wait_recv()
        _, _, col, width = self.parts[q]
        cols = pl.ds(col, width)
        far = self.two[0]
        own = self.one[2][self.t.pos(second, sign), :, cols]
        far[:, cols] = (far[:, cols].astype(jnp.float32) + own.astype(jnp.float32)).astype(far.dtype)
        self._copy(q, 1, 2).start()

    def total(self, q):
        _, second, _ = PATTERNS[RS_PARTS[q]]
        self._copy(q, 1, 1).wait_recv()
        self._copy(q, 1, 2).wait_recv()
        _, _, col, width = self.parts[q]
        cols = pl.ds(col, width)
        _, near, run = self.two
        own = self.one[2][self.t.pos(second), :, cols]
        return run[:, cols].astype(jnp.float32) + near[:, cols].astype(jnp.float32) + own.astype(jnp.float32)

    def drain(self, q):
        for stage in range(2):
            for kind in range(3):
                self._copy(q, stage, kind).wait_send()


class AllGather:
    def __init__(self, torus, buf, send_sems, recv_sems):
        self.t, self.buf = torus, buf
        self.send_sems, self.recv_sems = send_sems, recv_sems
        self.width = buf.shape[3] // len(PATTERNS)

    def _copy(self, q, inst, kind, receive=False):
        first, second, sign = PATTERNS[q]
        axis = first if inst == 0 else second
        offset = {first: 0 if inst == 0 else inst - 1, second: 0}
        if receive:
            offset[axis] = (-sign, sign, -2 * sign)[kind]
        elif kind == 2:
            offset[axis] = -sign
        piece = self.buf.at[self.t.pos('y', offset['y']), self.t.pos('x', offset['x']), :, pl.ds(q * self.width, self.width)]
        index = (q * (self.t.side + 1) + inst) * 3 + kind
        return remote(piece, piece, self.send_sems.at[index], self.recv_sems.at[index],
                      self.t.dev(axis, -sign if kind == 1 else sign))

    def _start(self, q, inst):
        self._copy(q, inst, 0).start()
        self._copy(q, inst, 1).start()

    def begin(self, q):
        self._start(q, 0)
        self._start(q, 1)

    def near(self, q):
        sign = PATTERNS[q][2]
        self._copy(q, 0, 0, True).wait_recv()
        self._copy(q, 0, 2).start()
        self._start(q, 1 + (-sign) % self.t.side)
        self._copy(q, 0, 1, True).wait_recv()
        self._start(q, 1 + sign % self.t.side)

    def far(self, q):
        self._copy(q, 0, 2, True).wait_recv()
        self._start(q, 1 + 2)

    def relay(self, q, j):
        self._copy(q, 1 + j, 0, True).wait_recv()
        self._copy(q, 1 + j, 2).start()

    def finish(self, q, j):
        self._copy(q, 1 + j, 1, True).wait_recv()
        self._copy(q, 1 + j, 2, True).wait_recv()

    def drain(self, q):
        for inst in range(self.t.side + 1):
            for kind in range(3):
                self._copy(q, inst, kind).wait_send()


NQ = len(PATTERNS)
NP = len(RS_PARTS)


def rs_kernel(side, part_hbm, rank_hbm, sum_ref, rank_sum_ref, part, rank, other, other_rank, far, near, run, far2, near2, run2,
              load_sems, pair_sems, send_sems, recv_sems):
    t = Torus(side)
    rounds, width = part.shape[0], part.shape[-1]
    share = width // NQ
    t.barrier()

    def loads(r):
        return (pltpu.make_async_copy(part_hbm.at[t.core, r], part.at[r], load_sems.at[0, r]),
                pltpu.make_async_copy(rank_hbm.at[t.core, r], rank.at[r], load_sems.at[1, r]),
                remote(part_hbm.at[1 - t.core, r], other.at[r], pair_sems.at[0, r], pair_sems.at[1, r], t.partner()),
                remote(rank_hbm.at[1 - t.core, r], other_rank.at[r], pair_sems.at[2, r], pair_sems.at[3, r], t.partner()))

    for r in range(rounds):
        for copy in loads(r):
            copy.start()

    def round_of(r):
        parts = [(part.at[r], q * share, q * share, share) for q in range(NQ)]
        parts.append((rank.at[r], 0, width, rank.shape[-1]))
        return ReduceScatter(t, parts, far.at[r], near.at[r], run.at[r], far2.at[r], near2.at[r], run2.at[r],
                             send_sems.at[r], recv_sems.at[r])

    rs = [round_of(r) for r in range(rounds)]

    def start(r):
        own, own_rank, pair, pair_rank = loads(r)
        own.wait()
        pair.wait_recv()
        own_rank.wait()
        pair_rank.wait_recv()

        @pl.loop(0, side)
        def _(i):
            for ref, more in ((part, other), (rank, other_rank)):
                ref[r, i] = (ref[r, i].astype(jnp.float32) + more[r, i].astype(jnp.float32)).astype(ref.dtype)

        for q in range(NP):
            rs[r].begin(q)

    def each(method, r):
        for q in range(NP):
            getattr(rs[r], method)(q)

    def finish(r):
        for q in range(NQ):
            sum_ref[r, :, pl.ds(q * share, share)] = rs[r].total(q)
        rank_sum_ref[r] = rs[r].total(NQ)

    start(0)
    for r in range(rounds):
        if r + 1 < rounds:
            start(r + 1)
        each('relay', r)
        if r > 0:
            each('relay_two', r - 1)
        each('turn', r)
        if r > 0:
            finish(r - 1)
    each('relay_two', rounds - 1)
    finish(rounds - 1)
    for r in range(rounds):
        each('drain', r)
        for copy in loads(r)[2:]:
            copy.wait_send()


def reduce_scatter(part, rank, side):
    cores, rounds, tokens, width = part.shape
    lanes = rank.shape[-1]
    rows = tokens // (side * side)
    dtype = part.dtype
    grid4 = (side, side, rows)
    scratch = [pltpu.VMEM((rounds,) + grid4 + (width,), dtype), pltpu.VMEM((rounds,) + grid4 + (lanes,), dtype)] * 2
    scratch += [pltpu.VMEM((rounds, side, rows, width + lanes), dtype)] * 3
    scratch += [pltpu.VMEM((rounds, rows, width + lanes), dtype)] * 3
    sems = NP * 6
    scratch += [pltpu.SemaphoreType.DMA((2, rounds)), pltpu.SemaphoreType.DMA((4, rounds)),
                pltpu.SemaphoreType.DMA((rounds, sems)), pltpu.SemaphoreType.DMA((rounds, sems))]
    return pl.pallas_call(
        functools.partial(rs_kernel, side),
        out_shape=(jax.ShapeDtypeStruct((rounds, rows, width), jnp.float32),
                   jax.ShapeDtypeStruct((rounds, rows, lanes), jnp.float32)),
        in_specs=[pl.BlockSpec(memory_space=pl.ANY)] * 2,
        out_specs=(pl.BlockSpec(memory_space=pltpu.VMEM),) * 2,
        scratch_shapes=scratch,
        compiler_params=pltpu.CompilerParams(collective_id=0, has_side_effects=True, vmem_limit_bytes=64 * 1024 * 1024 - 65536),
        name='reduce_scatter_tokens',
    )(part.reshape((cores, rounds) + grid4 + (width,)), rank.reshape((cores, rounds) + grid4 + (lanes,)))


def ag_kernel(side, shard_hbm, out_hbm, buf, load_sems, store_sems, pair_sems, send_sems, recv_sems):
    t = Torus(side)
    rounds = buf.shape[0]
    t.barrier()

    def load(r):
        return pltpu.make_async_copy(shard_hbm.at[r], buf.at[r, t.y, t.x], load_sems.at[r])

    def store(r):
        return pltpu.make_async_copy(buf.at[r], out_hbm.at[t.core, r], store_sems.at[r])

    def pair(r):
        return remote(buf.at[r], out_hbm.at[t.core, r], pair_sems.at[0, r], pair_sems.at[1, r], t.partner())

    def pair_in(r):
        return remote(buf.at[r], out_hbm.at[1 - t.core, r], pair_sems.at[0, r], pair_sems.at[1, r], t.partner())

    for r in range(rounds):
        load(r).start()
    ag = [AllGather(t, buf.at[r], send_sems.at[r], recv_sems.at[r]) for r in range(rounds)]

    def begin(r):
        load(r).wait()
        for q in range(NQ):
            ag[r].begin(q)

    begin(0)
    begin(1)
    for r in range(rounds):
        for q in range(NQ):
            ag[r].near(q)
        for q in range(NQ):
            ag[r].far(q)
        if r + 2 < rounds:
            begin(r + 2)
        for j in (0, 1, 3, 2):
            for q in range(NQ):
                ag[r].relay(q, j)
        for j in (0, 1, 3, 2):
            for q in range(NQ):
                ag[r].finish(q, j)
        store(r).start()
        pair(r).start()
    for r in range(rounds):
        for q in range(NQ):
            ag[r].drain(q)
        store(r).wait()
        pair(r).wait_send()
        pair_in(r).wait_recv()


def all_gather(shard, side):
    rounds, rows, width = shard.shape
    grid4 = (side, side, rows)
    sems = NQ * (side + 1) * 3
    out = pl.pallas_call(
        functools.partial(ag_kernel, side),
        out_shape=jax.ShapeDtypeStruct((CORES, rounds) + grid4 + (width,), shard.dtype),
        in_specs=[pl.BlockSpec(memory_space=pl.ANY)],
        out_specs=pl.BlockSpec(memory_space=pl.ANY),
        scratch_shapes=[pltpu.VMEM((rounds,) + grid4 + (width,), shard.dtype), pltpu.SemaphoreType.DMA((rounds,)),
                        pltpu.SemaphoreType.DMA((rounds,)), pltpu.SemaphoreType.DMA((2, rounds)),
                        pltpu.SemaphoreType.DMA((rounds, sems)), pltpu.SemaphoreType.DMA((rounds, sems))],
        compiler_params=pltpu.CompilerParams(collective_id=1, has_side_effects=True, vmem_limit_bytes=64 * 1024 * 1024 - 65536),
        name='all_gather_tokens',
    )(shard)
    return out.reshape(CORES, rounds, side * side * rows, width)


def rms_scale(x_in, gain_vec):
    x_f32 = x_in.astype(jnp.float32)
    inv_rms = lax.rsqrt(jnp.mean(x_f32 * x_f32, axis=-1, keepdims=True) + RMS_EPS)
    return (x_f32 * inv_rms * gain_vec).astype(jnp.bfloat16)


def causal_attention(q_flat, k_flat, v_flat, kv_heads, head_dim):
    num_seqs, seq_len = q_flat.shape[0], q_flat.shape[1]
    q_group = q_flat.reshape(num_seqs, seq_len, kv_heads, -1, head_dim)
    k_group = k_flat.reshape(num_seqs, seq_len, kv_heads, head_dim)
    v_group = v_flat.reshape(num_seqs, seq_len, kv_heads, head_dim)
    scores = jnp.einsum('bqngd,bknd->bngqk', q_group, k_group, preferred_element_type=jnp.float32) * head_dim ** -0.5
    causal = jnp.arange(seq_len)[:, None] >= jnp.arange(seq_len)[None, :]
    prob_bf = jax.nn.softmax(jnp.where(causal, scores, -jnp.inf), axis=-1).astype(jnp.bfloat16)
    att_out = jnp.einsum('bngqk,bknd->bqngd', prob_bf, v_group, preferred_element_type=jnp.float32)
    return att_out.astype(jnp.bfloat16).reshape(num_seqs, seq_len, -1)


def solution(mesh):
    act_spec = P('dp', None, None)
    w_head_spec = P(None, 'tp', None)
    w_out_spec = P('tp', None, None)
    w_col_spec = P(None, 'tp')
    w_row_spec = P('tp', None)
    a_rank_spec = P(None, None, 'tp')
    b_head_spec = P(None, None, 'tp', None)
    b_col_spec = P(None, None, 'tp')
    a_head_spec = P(None, 'tp', None, None)
    a_row_spec = P(None, 'tp', None)
    in_specs = (act_spec, P('dp'), P(None), P(None), w_head_spec, w_head_spec, w_head_spec, w_out_spec,
                w_col_spec, w_col_spec, w_row_spec, a_rank_spec, b_head_spec, a_rank_spec, b_head_spec,
                a_rank_spec, b_head_spec, a_head_spec, b_col_spec, a_rank_spec, b_col_spec,
                a_rank_spec, b_col_spec, a_row_spec, b_col_spec)
    devices = mesh.shape['tp']
    side = round((devices // CORES) ** 0.5)

    def local_layer(x_in, adapter_ids, gain_attn, gain_mlp, w_q, w_k, w_v, w_o, w_gate, w_up, w_down,
                    a_q, b_q, a_k, b_k, a_v, b_v, a_o, b_o, a_gate, b_gate, a_up, b_up, a_down, b_down):
        num_seqs, seq_len, model_dim = x_in.shape
        rank = b_q.shape[1]
        scale = LORA_ALPHA / rank
        rounds = num_seqs // CORES
        rows = seq_len // (devices // CORES)
        me = lax.axis_index('tp')
        core, chip = me % CORES, me // CORES

        a_mine = jnp.stack([a_q, a_k, a_v, a_gate, a_up]).reshape(5, -1, model_dim).transpose(1, 0, 2)
        b_mine = jnp.stack([b_o, b_down]).transpose(1, 2, 0, 3)
        a_all = lax.all_gather(a_mine, 'tp', axis=2, tiled=False)
        b_all = lax.all_gather(b_mine, 'tp', axis=3, tiled=True)

        def per_sequence(stack):
            return jnp.take(stack, adapter_ids, axis=0)

        a_seq = per_sequence(a_all)

        def column(h_in, w_locs, which, b_stacks):
            a_sel = a_seq[:, which[0]:which[1]].reshape(num_seqs, -1, model_dim)
            mid = jnp.einsum('bsd,brd->bsr', h_in, a_sel, preferred_element_type=jnp.float32).astype(jnp.bfloat16)
            outs = []
            for i, (w_loc, b_stack) in enumerate(zip(w_locs, b_stacks)):
                base = jnp.einsum('bsd,de->bse', h_in, w_loc.reshape(model_dim, -1), preferred_element_type=jnp.float32)
                low = jnp.einsum('bsr,bre->bse', mid[:, :, i * rank:(i + 1) * rank],
                                 per_sequence(b_stack).reshape(num_seqs, rank, -1), preferred_element_type=jnp.float32)
                outs.append((base + scale * low).astype(jnp.bfloat16))
            return outs

        def mine(full):
            rows_of = full.reshape((CORES, rounds, devices // CORES, rows) + full.shape[2:])
            rows_of = lax.dynamic_slice_in_dim(rows_of, core, 1, axis=0)[0]
            return lax.dynamic_slice_in_dim(rows_of, chip, 1, axis=1)[:, 0]

        def row_proj(h_in, w_loc, a_stack, b_full, resid):
            part = jnp.einsum('bse,ed->bsd', h_in, w_loc, preferred_element_type=jnp.float32).astype(jnp.bfloat16)
            mid = jnp.einsum('bse,ber->bsr', h_in, per_sequence(a_stack).reshape(num_seqs, -1, rank),
                             preferred_element_type=jnp.float32).astype(jnp.bfloat16)
            mid = jnp.pad(mid, ((0, 0), (0, 0), (0, LANES - rank)))
            split = (CORES, rounds, seq_len)
            total, mid_total = reduce_scatter(part.reshape(split + (model_dim,)), mid.reshape(split + (LANES,)), side)
            ids = lax.dynamic_slice_in_dim(adapter_ids, core * rounds, rounds, axis=0)
            low = jnp.einsum('bsr,brd->bsd', mid_total[:, :, :rank].astype(jnp.bfloat16), jnp.take(b_full, ids, axis=0),
                             preferred_element_type=jnp.float32)
            return (resid.astype(jnp.float32) + (total + scale * low)).astype(jnp.bfloat16)

        def whole(shard):
            return all_gather(shard, side).reshape(num_seqs, seq_len, model_dim)

        h_norm = rms_scale(x_in, gain_attn)
        q_loc, k_loc, v_loc = column(h_norm, (w_q, w_k, w_v), (0, 3), (b_q, b_k, b_v))
        att_loc = causal_attention(q_loc, k_loc, v_loc, w_k.shape[1], w_k.shape[2])
        x_one = row_proj(att_loc, w_o.reshape(-1, model_dim), a_o, b_all[:, :, 0], mine(x_in))
        h_two = whole(rms_scale(x_one, gain_mlp))
        gate_loc, up_loc = column(h_two, (w_gate, w_up), (3, 5), (b_gate, b_up))
        mlp_mid = (jax.nn.silu(gate_loc.astype(jnp.float32)) * up_loc.astype(jnp.float32)).astype(jnp.bfloat16)
        return whole(row_proj(mlp_mid, w_down, a_down, b_all[:, :, 1], x_one))

    return jax.shard_map(local_layer, mesh=mesh, in_specs=in_specs, out_specs=act_spec, check_vma=False)
```

time: 1360 us -> 833 us (0.61)
  waiting for transfers between devices: 730 us -> 53.3 us
  Pallas kernels: 0 us -> 440 us
  blocking collectives: 160 us -> 0 us
  local copies, waits for them, and re-layouts: 179 us -> 74.7 us
  matrix products: 231 us -> 209 us
    pallas_call x0 -> x4, Pallas kernels: none -> 440 us  [the longest x2 223 us: all_gather(): pl.pallas_call(functools.partial(ag_kernel, side), out_shape=jax.ShapeDty...]
    unnamed x8 -> x2, waiting for transfers between devices: 313 us -> 0.11 us
    all_gather x2, waiting for transfers between devices: 236 us -> 53.2 us  [the longest x1 38.8 us: local_layer(): a_all = lax.all_gather(a_mine, 'tp', axis=2, tiled=False)]
    psum x2 -> x0, waiting for transfers between devices: 182 us -> none  [row_proj(): value_a8 = lax.psum(value_a9, 'tp')]
    all_gather x5 -> x0, blocking collectives: 160 us -> none  [column_proj(): value_a8 = lax.all_gather(value_a9, 'tp', axis=2, tiled=True)]
    unnamed x63 -> x37, local copies, waits for them, and re-layouts: 169 us -> 31.1 us
    dot_general x17 -> x15, matrix products: 177 us -> 148 us  [the longest x4 98.2 us: column(): jnp.einsum('bsd,de->bse', h_in, w_loc.reshape(model_dim, -1), preferred_e...]
  transfers between devices with their start and end apart: 6 -> 2, of which waited for: 6 -> 2; matrix products, arithmetic and copies ran while one was open for 1% -> 4% of each run, Pallas kernels for 0% -> 0%
where the time goes in v1:
time: 833 us; the launch traced here: 822 us
  Pallas kernels  440 us (53%)
  matrix products  209 us (25%)
  local copies, waits for them, and re-layouts  74.7 us (9%)
  waiting for transfers between devices  53.3 us (6%)
  other arithmetic  31 us (4%)
  between operations  13.9 us (2%)
    pallas_call x2, Pallas kernels, all_gather(): pl.pallas_call(functools.partial(ag_kernel, side), out_shape=jax.ShapeDty...  223 us
    pallas_call x2, Pallas kernels, reduce_scatter(): pl.pallas_call(functools.partial(rs_kernel, side), out_shape=(jax.ShapeDt...  217 us
    dot_general x4, matrix products, column(): jnp.einsum('bsd,de->bse', h_in, w_loc.reshape(model_dim, -1), preferred_e...  98.2 us
    all_gather x1, waiting for transfers between devices, local_layer(): a_all = lax.all_gather(a_mine, 'tp', axis=2, tiled=False)  38.8 us
    dot_general x2, matrix products, row_proj(): jnp.einsum('bse,ed->bsd', h_in, w_loc, preferred_element_type=jnp.float32)  38.6 us
    dot_general x2, matrix products, column(): jnp.einsum('bsd,brd->bsr', h_in, a_sel, preferred_element_type=jnp.float32)  32.2 us
    unnamed x37, local copies, waits for them, and re-layouts  31.1 us
    gather x8, local copies, waits for them, and re-layouts, per_sequence(): return jnp.take(stack, adapter_ids, axis=0)  19.8 us
  transfers between devices with their start and end apart: 2, of which 2 were waited for; matrix products, arithmetic and copies ran while one was open for 4% of the time, Pallas kernels for 0%

profile of v1, /device:TPU:97, one launch (start us, length us, event | category | flops | bytes accessed | tf_op | source)
XLA Modules:
  0.0 822.2 jit_solution(7440323023546936541)
XLA Ops:
  18.7 2.1 gather_fusion.2
  20.9 2.1 gather_fusion.8
  23.0 2.1 gather_fusion.7
  27.1 11.3 %fusion = f32[8,512]{1,0:T(8,128)S(1)} fusion(bf16[8,512,4096]{2,1,0:T(8,128)(2,1)} %param.31), kind=kLoop, calls=%fused_computation.12 | loop fusion | flops 50327552 | bytes 33570816 | tf_op jit(solution)/shard_map/reduce_sum | solution.py:354
  38.5 14.5 %all-gather.4.cloned.1.call-done = bf16[4,32,2,4096]{3,1,0,2:T(8,128)(2,1)} async-done(((bf16[4,32,2,128]{3,1,0,2:T(8,128)(2,1)}), bf16[4,32,2,4096]{3,1,0,2:T(8,128)(2,1)}) %all-gather.4.cloned.1.call-update) | async-done | bytes 2097168 | tf_op jit(solution)/shard_map/all_gather | solution.py:401
  52.9 1.7 slice_bitcast_fusion
  57.8 38.8 %all-gather.6.cloned.1.call-done = bf16[4,5,131072]{2,0,1:T(4,128)(2,1)} async-done(((bf16[4,5,4096]{2,0,1:T(4,128)(2,1)}), bf16[4,5,131072]{2,0,1:T(4,128)(2,1)}) %all-gather.6.cloned.1.call-update) | async-done | bytes 5242896 | tf_op jit(solution)/shard_map/all_gather | solution.py:400
  96.6 8.2 reshape.219
  104.8 8.1 gather_fusion
  112.9 9.1 %broadcast_select_fusion = bf16[8,5,32,4096]{3,2,1,0:T(8,128)(2,1)} fusion(bf16[8,5,32,4096]{3,2,1,0:T(8,128)(2,1)} %gather_fusion, pred[8]{0:T(512)(128)(4,1)S(1)} %compare_and_fusion.1), kind=kLoop, calls=%fused_computation.17 | loop fusion | flops 5242880 | bytes 20971528 | tf_op jit(solution)/shard_map/jit(_take)/select_n | solution.py:404
  122.1 4.8 slice.72
  126.8 2.8 slice-done
  129.6 15.6 %fusion.44 = bf16[8,512,96]{1,2,0:T(8,128)(2,1)S(1)} fusion(bf16[8,96,4096]{2,1,0:T(8,128)(2,1)S(1)} %bitcast.142, bf16[8,512,4096]{2,1,0:T(8,128)(2,1)} %param.31, f32[4096]{0:T(1024)S(1)} %copy-done.14, f32[8,512]{1,0:T(8,128)S(1)} %add_rsqrt_fusion), kind=kOutput, calls=%fused_computation.59 | convolution fusion | flops 3288727552 | bytes 40665088 | tf_op jit(solution)/shard_map/bsd,brd->bsr/dot_general | solution.py:410
  147.1 16.3 %add_convert_fusion.2 = bf16[8,512,128]{1,2,0:T(8,128)(2,1)} fusion(f32[8,512,128]{1,2,0:T(8,128)S(1)} %fusion.69, bf16[8,512,4096]{2,1,0:T(8,128)(2,1)} %param.31, f32[4096]{0:T(1024)S(1)} %copy-done.14, f32[8,512]{1,0:T(8,128)S(1)} %add_rsqrt_fusion, bf16[4096,1,128]{2,0,1:T(8,128)(2,1)S(1)} %copy-done.12), kind=kOutput, calls=%fused_computation.55 | convolution fusion | flops 4363649024 | bytes 37781504 | tf_op jit(solution)/shard_map/bsd,de->bse/dot_general | solution.py:413
  163.4 16.6 %add_convert_fusion.4 = bf16[8,512,128]{1,2,0:T(8,128)(2,1)} fusion(f32[8,512,128]{1,2,0:T(8,128)S(1)} %fusion.73, bf16[8,512,4096]{2,1,0:T(8,128)(2,1)} %param.31, f32[4096]{0:T(1024)S(1)} %copy-done.14, f32[8,512]{1,0:T(8,128)S(1)} %add_rsqrt_fusion, bf16[4096,1,128]{2,0,1:T(8,128)(2,1)S(1)} %copy-done.13), kind=kOutput, calls=%fused_computation.57 | convolution fusion | flops 4363649024 | bytes 37781504 | tf_op jit(solution)/shard_map/bsd,de->bse/dot_general | solution.py:413
  180.1 18.9 %fusion.12 = (f32[8,512]{1,0:T(8,128)S(1)}, f32[8,512,512]{2,1,0:T(8,128)}) fusion(pred[512,512]{0,1:T(8,128)(4,1)S(1)} %iota_compare_fusion, bf16[8,512,128]{1,2,0:T(8,128)(2,1)} %add_convert_fusion.2, f32[8,512,128]{1,2,0:T(8,128)S(1)} %fusion.71, bf16[8,512,4096]{2,1,0:T(8,128)(2,1)} %param.31, f32[4096]{0:T(1024)S(1)} %copy-done.14, ...), kind=kOutput, calls=%fused_computation.28 | convolution fusion | flops 4906807296 | bytes 46448640 | tf_op jit(solution)/shard_map/bqngd,bknd->bngqk/dot_general | solution.py:363
  199.0 5.3 fusion.11
  204.8 4.0 fusion.47
  209.6 14.3 %convolution_convert_fusion.1 = bf16[8,512,4096]{2,1,0:T(8,128)(2,1)} fusion(bf16[8,512,128]{1,2,0:T(8,128)(2,1)S(1)} %fusion.47, bf16[1,128,4096]{2,1,0:T(8,128)(2,1)S(1)} %copy-done.4), kind=kOutput, calls=%fused_computation.16 | convolution fusion | flops 4311744512 | bytes 35651584 | tf_op jit(solution)/shard_map/bse,ed->bsd/dot_general | solution.py:425
  225.1 108.3 %reduce_scatter_tokens.2 = (f32[4,32,4096]{2,1,0:T(8,128)}, f32[4,32,128]{2,1,0:T(8,128)}) custom-call(bf16[2,4,4,4,32,4096]{5,4,3,2,1,0:T(8,128)(2,1)} %bitcast.140, bf16[2,4,4,4,32,128]{5,4,3,2,1,0:T(8,128)(2,1)} %bitcast.147), custom_call_target="tpu_custom_call" | custom-call | tf_op jit(solution)/shard_map/reduce_scatter_tokens/pallas_call | solution.py:271
  333.4 2.9 multiply_reduce_fusion
  338.9 112.3 %all_gather_tokens.2 = bf16[2,4,4,4,32,4096]{5,4,3,2,1,0:T(8,128)(2,1)} custom-call(bf16[4,32,4096]{2,1,0:T(8,128)(2,1)} %multiply_convert_fusion.shard_hbm), custom_call_target="tpu_custom_call" | custom-call | tf_op jit(solution)/shard_map/all_gather_tokens/pallas_call | solution.py:338
  451.3 16.5 %convolution_convert_fusion.2 = bf16[8,512,64]{1,2,0:T(8,128)(2,1)S(1)} fusion(bf16[8,512,4096]{2,1,0:T(8,128)(2,1)} %bitcast.137, bf16[8,64,4096]{2,1,0:T(8,128)(2,1)} %bitcast.145), kind=kOutput, calls=%fused_computation.61 | convolution fusion | flops 2147745792 | bytes 38273024 | tf_op jit(solution)/shard_map/bsd,brd->bsr/dot_general | solution.py:410
  467.8 3.8 fusion.65
  471.6 3.8 fusion.67
  475.4 18.8 %fusion.33 = f32[8,512,344]{1,2,0:T(8,128)} fusion(bf16[8,512,4096]{2,1,0:T(8,128)(2,1)} %bitcast.138, bf16[4096,344]{0,1:T(8,128)(2,1)S(1)} %copy-done.11), kind=kOutput, calls=%fused_computation.51 | convolution fusion | flops 11542724608 | bytes 42008576 | tf_op jit(solution)/shard_map/bsd,de->bse/dot_general | solution.py:413
  494.2 46.5 %fusion.17 = bf16[8,512,344]{1,2,0:T(8,128)(2,1)S(1)} fusion(f32[8,512,344]{1,2,0:T(8,128)} %fusion.33, f32[8,512,344]{1,2,0:T(8,128)} %fusion.67, f32[8,512,344]{1,2,0:T(8,128)} %fusion.65, bf16[8,512,4096]{2,1,0:T(8,128)(2,1)} %bitcast.139, bf16[4096,344]{0,1:T(8,128)(2,1)} %param.40), kind=kOutput, calls=%fused_computation.35 | convolution fusion | flops 11562450944 | bytes 56098816 | tf_op jit(solution)/shard_map/bsd,de->bse/dot_general | solution.py:413
  544.6 24.3 %convolution_convert_fusion = bf16[8,512,4096]{2,1,0:T(8,128)(2,1)} fusion(bf16[8,512,344]{1,2,0:T(8,128)(2,1)} %copy-done.3, bf16[344,4096]{1,0:T(8,128)(2,1)} %param.41), kind=kOutput, calls=%fused_computation.15 | convolution fusion | flops 11559501824 | bytes 39190528 | tf_op jit(solution)/shard_map/bse,ed->bsd/dot_general | solution.py:425
  568.9 108.3 %reduce_scatter_tokens.3 = (f32[4,32,4096]{2,1,0:T(8,128)}, f32[4,32,128]{2,1,0:T(8,128)}) custom-call(bf16[2,4,4,4,32,4096]{5,4,3,2,1,0:T(8,128)(2,1)} %bitcast.144, bf16[2,4,4,4,32,128]{5,4,3,2,1,0:T(8,128)(2,1)} %bitcast.146), custom_call_target="tpu_custom_call" | custom-call | tf_op jit(solution)/shard_map/reduce_scatter_tokens/pallas_call | solution.py:271
  677.2 4.0 fusion.24.shard_hbm
  681.3 110.9 %all_gather_tokens.3 = bf16[2,4,4,4,32,4096]{5,4,3,2,1,0:T(8,128)(2,1)} custom-call(bf16[4,32,4096]{2,1,0:T(8,128)(2,1)} %fusion.24.shard_hbm), custom_call_target="tpu_custom_call" | custom-call | tf_op jit(solution)/shard_map/all_gather_tokens/pallas_call | solution.py:338
  792.2 22.9 %copy.54 = bf16[8,512,4096]{2,1,0:T(8,128)(2,1)} copy(bf16[8,512,4096]{2,1,0:T(8,128)(2,1)} %bitcast.141) | data formatting | bytes 67108864
  (65 shorter events, 28.1 us)
Async XLA Ops:
  6.5 46.4 %all-gather.4.cloned.1.call-start = ((), (), s32[]{:S(2)}) async-start(), calls=%async_computation | async-start | bytes 2162688 | tf_op jit(solution)/shard_map/all_gather | solution.py:401
  8.0 88.6 %all-gather.6.cloned.1.call-start = ((), (), s32[]{:S(2)}) async-start(), calls=%async_computation.1 | async-start | bytes 5406720 | tf_op jit(solution)/shard_map/all_gather | solution.py:400
  12.0 0.7 copy-start.7
  27.1 181.7 %copy-start.8 = (pred[8]{0:T(512)(128)(4,1)}, pred[8]{0:T(512)(128)(4,1)S(1)}, u32[]{:S(2)}) copy-start(pred[8]{0:T(512)(128)(4,1)S(1)} %compare_and_fusion.1) | copy-start | bytes 28
  126.8 2.8 slice-start
  126.8 2.8 copy-start.14
  145.2 1.9 copy-start.12
  147.1 16.3 %copy-start.13 = (bf16[4096,1,128]{2,0,1:T(8,128)(2,1)S(1)}, bf16[4096,1,128]{2,0,1:T(8,128)(2,1)}, u32[]{:S(2)}) copy-start(bf16[4096,1,128]{2,0,1:T(8,128)(2,1)} %param.37) | copy-start | bytes 3145732
  199.0 5.8 copy-start.1
  204.8 4.8 copy-start.4
  333.4 4.3 copy-start.10
  336.3 1.4 copy-start
  451.2 16.6 %copy-start.6 = (bf16[8,32,344]{2,1,0:T(8,128)(2,1)S(1)}, bf16[8,32,344]{2,1,0:T(8,128)(2,1)}, u32[]{:S(2)}) copy-start(bf16[8,32,344]{2,1,0:T(8,128)(2,1)} %gather_fusion.8) | copy-start | bytes 528388
  451.2 16.6 %copy-start.9 = (pred[8]{0:T(512)(128)(4,1)S(1)}, pred[8]{0:T(512)(128)(4,1)}, u32[]{:S(2)}) copy-start(pred[8]{0:T(512)(128)(4,1)} %copy-done.8) | copy-start | bytes 28
  467.8 3.8 copy-start.5
  467.8 7.6 copy-start.11
  494.2 48.1 %copy-start.2 = (bf16[8,344,32]{1,2,0:T(8,128)(2,1)S(1)}, bf16[8,344,32]{1,2,0:T(8,128)(2,1)}, u32[]{:S(2)}) copy-start(bf16[8,344,32]{1,2,0:T(8,128)(2,1)} %gather_fusion.2) | copy-start | bytes 528388
  540.7 1.6 copy-start.3
Sparse Core Ops, SparseCore 0:
  9.3 43.5 all-gather.3
  55.1 41.4 all-gather.5
